TPU v7x, 32 devices: a whole 2x2x4 slice. The times are simulated.
32 devices in a mesh: vox: 16 (over z, x, core), subj: 2 (over y).
Axes of the slice: x: 2, y: 2, z: 4, core: 2. Of those that a mesh axis runs over, the one named last changes fastest.
Arguments:
- series: bfloat16 [8, 4096, 512], P('subj', 'vox'), may hold values from -6 to 6
- live_mask: int32 [4096], P('vox'), may hold values from 0 to 1, as said below
- neighbours: int32 [4096, 13], P('vox'), may hold values from -1 to 510, as said below
- start_vectors: float32 [4096, 64], P('vox'), may hold values from -60 to 60
Outputs:
- embedding: float32 [4096, 64], P('vox')
Inputs may be any that keep to these rules, and one draw needn't show every extreme that they name: `live_mask`: within each aligned block of 128 voxel slots the live slots are a leading run of 1 to 128 slots. `neighbours`: slot n of voxel i names voxel (i // 256 - 1) * 256 + n, which is live and lies before i; the entries of a row are distinct or -1; rows of dead voxels are all -1; rows of the first 256 voxels name no slot under 256.
All inputs are finite; a program needn't handle non-finite values.
Results may differ from a plain program's by a relative error of at most 0.0024.
Values may be sent and summed in bfloat16 or wider, within the bound.
No kernel may reach another device: no remote copies, remote signals or barrier semaphores. Data moves between devices by JAX's collectives and lax.ppermute only.
A program may use at most 64 MiB of HBM per device.

v0:
```python
import math
import jax
import jax.numpy as jnp
from jax import lax
from jax.sharding import PartitionSpec as P

ITERS = 3


def shifted(shard, axis, by):
    count = lax.axis_size(axis)
    pairs = [(i, i + by) for i in range(count) if 0 <= i + by < count]
    return lax.ppermute(shard, axis, pairs)


def exchanged(value, axis, distance):
    count = lax.axis_size(axis)
    return lax.ppermute(value, axis, [(i, i ^ distance) for i in range(count)])


def summed_over(value, axis):
    count = lax.axis_size(axis)
    if count & count - 1:
        return lax.psum(value, axis)
    stride = 1
    while stride < count:
        if stride > 1 and 4 * stride <= count:
            first, second, third = (exchanged(value, axis, k * stride) for k in (1, 2, 3))
            value = value + first + (second + third)
            stride *= 4
        else:
            value = value + exchanged(value, axis, stride)
            stride *= 2
    return value


def as_sent(shard):
    return jax.tree.map(lambda a: a.astype(jnp.bfloat16) if a.dtype == jnp.float32 else a, shard)


def standard(block):
    values = block.astype(jnp.float32)
    center = values - jnp.mean(values, axis=-1, keepdims=True)
    spread = jnp.mean(center * center, axis=-1, keepdims=True)
    return (center * lax.rsqrt(spread + 1e-05)).astype(jnp.bfloat16)


def orthonormal(images):
    gram_matrix = jnp.dot(images.T, images, precision=lax.Precision.HIGHEST)
    gram_matrix = summed_over(gram_matrix, "vox")
    factor = jnp.linalg.cholesky(gram_matrix)
    return lax.linalg.triangular_solve(
        factor, images, left_side=False, lower=True, transpose_a=True
    )


def dense_graph(weight, slots, columns_total):
    column_ids = jnp.arange(columns_total, dtype=jnp.int32)
    matrix = jnp.zeros((weight.shape[0], columns_total), jnp.float32)
    for offset in range(weight.shape[1]):
        hits = (slots[:, offset][:, None] == column_ids[None, :]).astype(jnp.float32)
        matrix = matrix + weight[:, offset][:, None] * hits
    return matrix


def product(left, right):
    return jnp.dot(left, right, precision=lax.Precision.HIGHEST)


def on_device(series, live_mask, neighbours, start_vectors):
    voxels_here = series.shape[1]
    frames = series.shape[2]
    subjects = series.shape[0] * lax.axis_size("subj")
    scale_factor = 0.5 / math.sqrt(frames * subjects)
    zscored = standard(series)
    earlier = shifted(zscored, "vox", 1)
    window = jnp.concatenate([earlier, zscored], axis=1)
    present = neighbours >= 0
    safe_slots = jnp.maximum(neighbours, 0)
    columns = []
    for offset in range(neighbours.shape[1]):
        picked = jnp.take(window, safe_slots[:, offset], axis=1)
        columns.append(
            jnp.einsum("svf,svf->v", zscored, picked, preferred_element_type=jnp.float32)
        )
    partial_sums = jnp.stack(columns, axis=1)
    summed = lax.psum(partial_sums, "subj")
    weight = jnp.where(present, jnp.exp(scale_factor * summed), 0.0)
    living = live_mask.astype(jnp.float32)
    local_graph = dense_graph(weight, neighbours, 2 * voxels_here)
    owed = jnp.sum(local_graph, axis=0)
    received = shifted(owed[:voxels_here], "vox", -1)
    degree = 1.0 + jnp.sum(weight, axis=1) + owed[voxels_here:] + received
    scaling = living * lax.rsqrt(degree)
    vectors = living[:, None] * start_vectors
    for repeat in range(ITERS):
        scaled = scaling[:, None] * vectors
        earlier_rows = shifted(as_sent(scaled), "vox", 1).astype(scaled.dtype)
        window_rows = jnp.concatenate([earlier_rows, scaled], axis=0)
        forward = product(local_graph, window_rows)
        returns = product(local_graph.T, scaled)
        arrived = shifted(as_sent(returns[:voxels_here]), "vox", -1)
        images = 0.5 * (
            vectors + scaling[:, None] * (scaled + forward + returns[voxels_here:] + arrived)
        )
        vectors = orthonormal(images)
    return vectors


def solution(mesh):
    placed = (P("subj", "vox", None), P("vox"), P("vox", None), P("vox", None))
    return jax.shard_map(
        on_device, mesh=mesh, in_specs=placed, out_specs=P("vox", None), check_vma=False
    )
```

profile of v0, /device:TPU:0, one launch (start us, length us, event | category | flops | bytes accessed | tf_op | source)
XLA Modules:
  0.0 203.3 jit_solution(12058164480931716978)
XLA Ops:
  5.0 2.6 %collective-permute-start = (bf16[4,256,512]{2,0,1:T(4,128)(2,1)S(1)}, bf16[4,256,512]{2,0,1:T(4,128)(2,1)S(1)}, u32[]{:S(2)}, u32[]{:S(2)}) collective-permute-start(bf16[4,256,512]{2,0,1:T(4,128)(2,1)S(1)} %fusion.3), channel_id=1, source_target_pairs={{0,2},{2,4},{4,6},{6,8},{8,10},{10,12},{12,14},{14,16},{16,18},{18... | collective-permute-start | bytes 3145736 | tf_op jit(solution)/shard_map/ppermute | solution.py:13
  21.5 2.5 %gather_fusion.12 = bf16[256,4,512]{2,1,0:T(4,128)(2,1)} fusion(bf16[4,512,512]{2,0,1:T(4,128)(2,1)S(1)} %pad_maximum_fusion, s32[1024]{0:T(1024)S(1)} %pad_clamp_fusion), kind=kCustom, calls=%fused_computation.12.clone | custom fusion | bytes 2098176 | tf_op jit(solution)/shard_map/jit(_take)/gather | solution.py:82
  36.4 2.7 %gather_fusion.6 = bf16[256,4,512]{2,1,0:T(4,128)(2,1)} fusion(bf16[4,512,512]{2,0,1:T(4,128)(2,1)S(1)} %pad_maximum_fusion, s32[1024]{0:T(1024)S(1)} %pad_clamp_fusion.6), kind=kCustom, calls=%fused_computation.6.clone | custom fusion | bytes 2098176 | tf_op jit(solution)/shard_map/jit(_take)/gather | solution.py:82
  44.1 9.5 %fusion.7 = (f32[256]{0:T(256)S(1)}, f32[256]{0:T(256)S(1)}, f32[256]{0:T(256)S(1)}, f32[256]{0:T(256)S(1)}) fusion(bf16[256,4,512]{2,1,0:T(4,128)(2,1)} %gather_fusion.3, pred[256]{0:T(512)(128)(4,1)S(1)} %get-tuple-element.72, bf16[256,4,512]{2,1,0:T(4,128)(2,1)} %gather_fusion.2, pred[256]{0:T(512)(128)(4,1)S(1)} %get-tuple-element.73, ...), kind=kLoop, calls=%fused_computation.35 | loop fusion | flops 11009024 | bytes 5256192 | tf_op jit(solution)/shard_map/svf,svf->v/dot_general | solution.py:84
  53.7 14.7 %fusion.16 = (f32[256]{0:T(256)S(1)}, f32[256]{0:T(256)S(1)}, f32[256]{0:T(256)S(1)}, f32[256]{0:T(256)S(1)}, f32[256]{0:T(256)S(1)}, /*index=5*/f32[256]{0:T(25...) fusion(bf16[256,4,512]{2,1,0:T(4,128)(2,1)S(1)} %copy-done.1, pred[256]{0:T(512)(128)(4,1)S(1)} %get-tuple-element.76, ...), kind=kLoop, calls=%fused_computation.44 | loop fusion | flops 21493504 | bytes 10505472 | tf_op jit(solution)/shard_map/svf,svf->v/dot_general | solution.py:84
  68.5 9.0 %psum.7 = f32[256,13]{0,1:T(8,128)S(1)} all-reduce(f32[256,13]{0,1:T(8,128)S(1)} %stack.55), channel_id=1, replica_groups=mesh['vox'=16,'subj'=2] {'subj'}, use_global_device_ids=true, to_apply=%region_2.0 | all-reduce | flops 3328 | bytes 26624 | tf_op jit(solution)/shard_map/psum | solution.py:87
  79.8 9.8 %collective-permute-done.1 = f32[256]{0:T(256)S(1)} collective-permute-done((f32[256]{0:T(256)S(1)}, f32[256]{0:T(256)S(1)}, u32[]{:S(2)}, u32[]{:S(2)}) %collective-permute-start.1) | collective-permute-done | bytes 1056 | tf_op jit(solution)/shard_map/ppermute | solution.py:13
  89.6 7.1 %collective-permute-start.2 = (bf16[256,64]{0,1:T(8,128)(2,1)S(1)}, bf16[256,64]{0,1:T(8,128)(2,1)S(1)}, u32[]{:S(2)}, u32[]{:S(2)}) collective-permute-start(bf16[256,64]{0,1:T(8,128)(2,1)S(1)} %get-tuple-element.25), channel_id=1, source_target_pairs={{0,2},{2,4},{4,6},{6,8},{8,10},{10,12},{12,14},{14,16},{16,18},{18... | collective-permute-start | bytes 98312 | tf_op jit(solution)/shard_map/ppermute | solution.py:13
  101.1 2.9 %collective-permute-start.4 = (f32[64,64]{0,1:T(8,128)S(1)}, f32[64,64]{0,1:T(8,128)S(1)}, u32[]{:S(2)}, u32[]{:S(2)}) collective-permute-start(f32[64,64]{0,1:T(8,128)S(1)} %fusion.66), channel_id=1, source_target_pairs={{0,2},{2,0},{4,6},{6,4},{8,10},{10,8},{12,14},{14,12},{16,18},{18,... | collective-permute-start | bytes 49160 | tf_op jit(solution)/shard_map/ppermute | solution.py:18
  112.9 2.7 %collective-permute-start.8 = (f32[64,64]{0,1:T(8,128)S(1)}, f32[64,64]{0,1:T(8,128)S(1)}, u32[]{:S(2)}, u32[]{:S(2)}) collective-permute-start(f32[64,64]{0,1:T(8,128)S(1)} %add_add_fusion.2), channel_id=1, source_target_pairs={{0,16},{2,18},{4,20},{6,22},{8,24},{10,26},{12,28},{14,30},{16,0},... | collective-permute-start | bytes 49160 | tf_op jit(solution)/shard_map/ppermute | solution.py:18
  117.8 5.8 %cholesky.59 = f32[64,64]{1,0:T(8,128)S(1)} custom-call(f32[64,64]{1,0:T(8,128)S(1)} %fusion.49), custom_call_target="Cholesky" | custom-call | tf_op jit(solution)/shard_map/jit(cholesky)/cholesky | solution.py:51
  125.0 4.9 %custom-call.7 = f32[1,64,64]{1,2,0:T(8,128)S(1)} custom-call(f32[1,64,64]{2,1,0:T(8,128)S(1)} %fusion.41), custom_call_target="InvertDiagBlocksLowerTriangular" | custom-call | tf_op jit(solution)/shard_map/triangular_solve/custom-call.0 | solution.py:52
  133.6 3.2 %collective-permute-done.10 = bf16[256,64]{0,1:T(8,128)(2,1)S(1)} collective-permute-done((bf16[256,64]{0,1:T(8,128)(2,1)S(1)}, bf16[256,64]{0,1:T(8,128)(2,1)S(1)}, u32[]{:S(2)}, u32[]{:S(2)}) %collective-permute-start.10) | collective-permute-done | bytes 32800 | tf_op jit(solution)/shard_map/ppermute | solution.py:13
  137.6 2.7 %collective-permute-start.11 = (f32[64,64]{0,1:T(8,128)S(1)}, f32[64,64]{0,1:T(8,128)S(1)}, u32[]{:S(2)}, u32[]{:S(2)}) collective-permute-start(f32[64,64]{0,1:T(8,128)S(1)} %fusion.68), channel_id=1, source_target_pairs={{0,2},{2,0},{4,6},{6,4},{8,10},{10,8},{12,14},{14,12},{16,18},{18,... | collective-permute-start | bytes 49160 | tf_op jit(solution)/shard_map/ppermute | solution.py:18
  142.5 2.7 %collective-permute-start.14 = (f32[64,64]{0,1:T(8,128)S(1)}, f32[64,64]{0,1:T(8,128)S(1)}, u32[]{:S(2)}, u32[]{:S(2)}) collective-permute-start(f32[64,64]{0,1:T(8,128)S(1)} %add.187), channel_id=1, source_target_pairs={{0,12},{2,14},{4,8},{6,10},{8,4},{10,6},{12,0},{14,2},{16,28},{18,... | collective-permute-start | bytes 49160 | tf_op jit(solution)/shard_map/ppermute | solution.py:18
  150.3 3.7 %collective-permute-done.15 = f32[64,64]{0,1:T(8,128)S(1)} collective-permute-done((f32[64,64]{0,1:T(8,128)S(1)}, f32[64,64]{0,1:T(8,128)S(1)}, u32[]{:S(2)}, u32[]{:S(2)}) %collective-permute-start.15) | collective-permute-done | bytes 16416 | tf_op jit(solution)/shard_map/ppermute | solution.py:18
  154.1 5.8 %cholesky.70 = f32[64,64]{1,0:T(8,128)S(1)} custom-call(f32[64,64]{1,0:T(8,128)S(1)} %fusion.47), custom_call_target="Cholesky" | custom-call | tf_op jit(solution)/shard_map/jit(cholesky)/cholesky | solution.py:51
  161.3 4.9 %custom-call.8 = f32[1,64,64]{1,2,0:T(8,128)S(1)} custom-call(f32[1,64,64]{2,1,0:T(8,128)S(1)} %fusion.42), custom_call_target="InvertDiagBlocksLowerTriangular" | custom-call | tf_op jit(solution)/shard_map/triangular_solve/custom-call.0 | solution.py:52
  169.6 3.4 %collective-permute-done.17 = bf16[256,64]{0,1:T(8,128)(2,1)S(1)} collective-permute-done((bf16[256,64]{0,1:T(8,128)(2,1)S(1)}, bf16[256,64]{0,1:T(8,128)(2,1)S(1)}, u32[]{:S(2)}, u32[]{:S(2)}) %collective-permute-start.17) | collective-permute-done | bytes 32800 | tf_op jit(solution)/shard_map/ppermute | solution.py:13
  173.8 2.7 %collective-permute-start.18 = (f32[64,64]{0,1:T(8,128)S(1)}, f32[64,64]{0,1:T(8,128)S(1)}, u32[]{:S(2)}, u32[]{:S(2)}) collective-permute-start(f32[64,64]{0,1:T(8,128)S(1)} %fusion.70), channel_id=1, source_target_pairs={{0,2},{2,0},{4,6},{6,4},{8,10},{10,8},{12,14},{14,12},{16,18},{18,... | collective-permute-start | bytes 49160 | tf_op jit(solution)/shard_map/ppermute | solution.py:18
  178.7 2.7 %collective-permute-start.21 = (f32[64,64]{0,1:T(8,128)S(1)}, f32[64,64]{0,1:T(8,128)S(1)}, u32[]{:S(2)}, u32[]{:S(2)}) collective-permute-start(f32[64,64]{0,1:T(8,128)S(1)} %add.196), channel_id=1, source_target_pairs={{0,12},{2,14},{4,8},{6,10},{8,4},{10,6},{12,0},{14,2},{16,28},{18,... | collective-permute-start | bytes 49160 | tf_op jit(solution)/shard_map/ppermute | solution.py:18
  185.4 4.8 %collective-permute-done.22 = f32[64,64]{0,1:T(8,128)S(1)} collective-permute-done((f32[64,64]{0,1:T(8,128)S(1)}, f32[64,64]{0,1:T(8,128)S(1)}, u32[]{:S(2)}, u32[]{:S(2)}) %collective-permute-start.22) | collective-permute-done | bytes 16416 | tf_op jit(solution)/shard_map/ppermute | solution.py:18
  190.3 5.8 %cholesky.81 = f32[64,64]{1,0:T(8,128)S(1)} custom-call(f32[64,64]{1,0:T(8,128)S(1)} %fusion.45), custom_call_target="Cholesky" | custom-call | tf_op jit(solution)/shard_map/jit(cholesky)/cholesky | solution.py:51
  197.5 4.9 %custom-call.9 = f32[1,64,64]{1,2,0:T(8,128)S(1)} custom-call(f32[1,64,64]{2,1,0:T(8,128)S(1)} %fusion.43), custom_call_target="InvertDiagBlocksLowerTriangular" | custom-call | tf_op jit(solution)/shard_map/triangular_solve/custom-call.0 | solution.py:52
  (168 shorter events, 80.7 us)
Async XLA Ops:
  5.0 5.2 %collective-permute-start = (bf16[4,256,512]{2,0,1:T(4,128)(2,1)S(1)}, bf16[4,256,512]{2,0,1:T(4,128)(2,1)S(1)}, u32[]{:S(2)}, u32[]{:S(2)}) collective-permute-start(bf16[4,256,512]{2,0,1:T(4,128)(2,1)S(1)} %fusion.3), channel_id=1, source_target_pairs={{0,2},{2,4},{4,6},{6,8},{8,10},{10,12},{12,14},{14,16},{16,18},{18... | collective-permute-start | bytes 3145736 | tf_op jit(solution)/shard_map/ppermute | solution.py:13
  53.7 35.9 %copy-start.6 = (f32[256,64]{0,1:T(8,128)S(1)}, f32[256,64]{0,1:T(8,128)}, u32[]{:S(2)}) copy-start(f32[256,64]{0,1:T(8,128)} %param.12) | copy-start | bytes 196612
  78.5 11.1 %collective-permute-start.1 = (f32[256]{0:T(256)S(1)}, f32[256]{0:T(256)S(1)}, u32[]{:S(2)}, u32[]{:S(2)}) collective-permute-start(f32[256]{0:T(256)S(1)} %slice.190), channel_id=1, source_target_pairs={{2,0},{4,2},{6,4},{8,6},{10,8},{12,10},{14,12},{16,14},{18,16},{20... | collective-permute-start | bytes 3080 | tf_op jit(solution)/shard_map/ppermute | solution.py:13
  89.6 8.8 %collective-permute-start.2 = (bf16[256,64]{0,1:T(8,128)(2,1)S(1)}, bf16[256,64]{0,1:T(8,128)(2,1)S(1)}, u32[]{:S(2)}, u32[]{:S(2)}) collective-permute-start(bf16[256,64]{0,1:T(8,128)(2,1)S(1)} %get-tuple-element.25), channel_id=1, source_target_pairs={{0,2},{2,4},{4,6},{6,8},{8,10},{10,12},{12,14},{14,16},{16,18},{18... | collective-permute-start | bytes 98312 | tf_op jit(solution)/shard_map/ppermute | solution.py:13
  97.1 3.1 %collective-permute-start.3 = (bf16[256,64]{0,1:T(8,128)(2,1)S(1)}, bf16[256,64]{0,1:T(8,128)(2,1)S(1)}, u32[]{:S(2)}, u32[]{:S(2)}) collective-permute-start(bf16[256,64]{0,1:T(8,128)(2,1)S(1)} %slice.264), channel_id=1, source_target_pairs={{2,0},{4,2},{6,4},{8,6},{10,8},{12,10},{14,12},{16,14},{18,16},{20... | collective-permute-start | bytes 98312 | tf_op jit(solution)/shard_map/ppermute | solution.py:13
  101.1 3.8 %collective-permute-start.4 = (f32[64,64]{0,1:T(8,128)S(1)}, f32[64,64]{0,1:T(8,128)S(1)}, u32[]{:S(2)}, u32[]{:S(2)}) collective-permute-start(f32[64,64]{0,1:T(8,128)S(1)} %fusion.66), channel_id=1, source_target_pairs={{0,2},{2,0},{4,6},{6,4},{8,10},{10,8},{12,14},{14,12},{16,18},{18,... | collective-permute-start | bytes 49160 | tf_op jit(solution)/shard_map/ppermute | solution.py:18
  104.9 4.2 %collective-permute-start.6 = (f32[64,64]{0,1:T(8,128)S(1)}, f32[64,64]{0,1:T(8,128)S(1)}, u32[]{:S(2)}, u32[]{:S(2)}) collective-permute-start(f32[64,64]{0,1:T(8,128)S(1)} %add.178), channel_id=1, source_target_pairs={{0,8},{2,10},{4,12},{6,14},{8,0},{10,2},{12,4},{14,6},{16,24},{18,... | collective-permute-start | bytes 49160 | tf_op jit(solution)/shard_map/ppermute | solution.py:18
  106.6 4.8 %collective-permute-start.7 = (f32[64,64]{0,1:T(8,128)S(1)}, f32[64,64]{0,1:T(8,128)S(1)}, u32[]{:S(2)}, u32[]{:S(2)}) collective-permute-start(f32[64,64]{0,1:T(8,128)S(1)} %add.178), channel_id=1, source_target_pairs={{0,12},{2,14},{4,8},{6,10},{8,4},{10,6},{12,0},{14,2},{16,28},{18,... | collective-permute-start | bytes 49160 | tf_op jit(solution)/shard_map/ppermute | solution.py:18
  108.9 3.9 %collective-permute-start.5 = (f32[64,64]{0,1:T(8,128)S(1)}, f32[64,64]{0,1:T(8,128)S(1)}, u32[]{:S(2)}, u32[]{:S(2)}) collective-permute-start(f32[64,64]{0,1:T(8,128)S(1)} %add.178), channel_id=1, source_target_pairs={{0,4},{2,6},{4,0},{6,2},{8,12},{10,14},{12,8},{14,10},{16,20},{18,... | collective-permute-start | bytes 49160 | tf_op jit(solution)/shard_map/ppermute | solution.py:18
  112.9 4.9 %collective-permute-start.8 = (f32[64,64]{0,1:T(8,128)S(1)}, f32[64,64]{0,1:T(8,128)S(1)}, u32[]{:S(2)}, u32[]{:S(2)}) collective-permute-start(f32[64,64]{0,1:T(8,128)S(1)} %add_add_fusion.2), channel_id=1, source_target_pairs={{0,16},{2,18},{4,20},{6,22},{8,24},{10,26},{12,28},{14,30},{16,0},... | collective-permute-start | bytes 49160 | tf_op jit(solution)/shard_map/ppermute | solution.py:18
  130.2 3.3 %collective-permute-start.9 = (bf16[256,64]{0,1:T(8,128)(2,1)S(1)}, bf16[256,64]{0,1:T(8,128)(2,1)S(1)}, u32[]{:S(2)}, u32[]{:S(2)}) collective-permute-start(bf16[256,64]{0,1:T(8,128)(2,1)S(1)} %get-tuple-element.23), channel_id=1, source_target_pairs={{0,2},{2,4},{4,6},{6,8},{8,10},{10,12},{12,14},{14,16},{16,18},{18... | collective-permute-start | bytes 98312 | tf_op jit(solution)/shard_map/ppermute | solution.py:13
  132.0 4.8 %collective-permute-start.10 = (bf16[256,64]{0,1:T(8,128)(2,1)S(1)}, bf16[256,64]{0,1:T(8,128)(2,1)S(1)}, u32[]{:S(2)}, u32[]{:S(2)}) collective-permute-start(bf16[256,64]{0,1:T(8,128)(2,1)S(1)} %slice.263), channel_id=1, source_target_pairs={{2,0},{4,2},{6,4},{8,6},{10,8},{12,10},{14,12},{16,14},{18,16},{20... | collective-permute-start | bytes 98312 | tf_op jit(solution)/shard_map/ppermute | solution.py:13
  137.6 3.6 %collective-permute-start.11 = (f32[64,64]{0,1:T(8,128)S(1)}, f32[64,64]{0,1:T(8,128)S(1)}, u32[]{:S(2)}, u32[]{:S(2)}) collective-permute-start(f32[64,64]{0,1:T(8,128)S(1)} %fusion.68), channel_id=1, source_target_pairs={{0,2},{2,0},{4,6},{6,4},{8,10},{10,8},{12,14},{14,12},{16,18},{18,... | collective-permute-start | bytes 49160 | tf_op jit(solution)/shard_map/ppermute | solution.py:18
  141.2 4.1 %collective-permute-start.13 = (f32[64,64]{0,1:T(8,128)S(1)}, f32[64,64]{0,1:T(8,128)S(1)}, u32[]{:S(2)}, u32[]{:S(2)}) collective-permute-start(f32[64,64]{0,1:T(8,128)S(1)} %add.187), channel_id=1, source_target_pairs={{0,8},{2,10},{4,12},{6,14},{8,0},{10,2},{12,4},{14,6},{16,24},{18,... | collective-permute-start | bytes 49160 | tf_op jit(solution)/shard_map/ppermute | solution.py:18
  142.5 5.0 %collective-permute-start.14 = (f32[64,64]{0,1:T(8,128)S(1)}, f32[64,64]{0,1:T(8,128)S(1)}, u32[]{:S(2)}, u32[]{:S(2)}) collective-permute-start(f32[64,64]{0,1:T(8,128)S(1)} %add.187), channel_id=1, source_target_pairs={{0,12},{2,14},{4,8},{6,10},{8,4},{10,6},{12,0},{14,2},{16,28},{18,... | collective-permute-start | bytes 49160 | tf_op jit(solution)/shard_map/ppermute | solution.py:18
  145.2 3.9 %collective-permute-start.12 = (f32[64,64]{0,1:T(8,128)S(1)}, f32[64,64]{0,1:T(8,128)S(1)}, u32[]{:S(2)}, u32[]{:S(2)}) collective-permute-start(f32[64,64]{0,1:T(8,128)S(1)} %add.187), channel_id=1, source_target_pairs={{0,4},{2,6},{4,0},{6,2},{8,12},{10,14},{12,8},{14,10},{16,20},{18,... | collective-permute-start | bytes 49160 | tf_op jit(solution)/shard_map/ppermute | solution.py:18
  149.1 4.9 %collective-permute-start.15 = (f32[64,64]{0,1:T(8,128)S(1)}, f32[64,64]{0,1:T(8,128)S(1)}, u32[]{:S(2)}, u32[]{:S(2)}) collective-permute-start(f32[64,64]{0,1:T(8,128)S(1)} %add_add_fusion.1), channel_id=1, source_target_pairs={{0,16},{2,18},{4,20},{6,22},{8,24},{10,26},{12,28},{14,30},{16,0},... | collective-permute-start | bytes 49160 | tf_op jit(solution)/shard_map/ppermute | solution.py:18
  166.5 3.1 %collective-permute-start.16 = (bf16[256,64]{0,1:T(8,128)(2,1)S(1)}, bf16[256,64]{0,1:T(8,128)(2,1)S(1)}, u32[]{:S(2)}, u32[]{:S(2)}) collective-permute-start(bf16[256,64]{0,1:T(8,128)(2,1)S(1)} %get-tuple-element.21), channel_id=1, source_target_pairs={{0,2},{2,4},{4,6},{6,8},{8,10},{10,12},{12,14},{14,16},{16,18},{18... | collective-permute-start | bytes 98312 | tf_op jit(solution)/shard_map/ppermute | solution.py:13
  168.3 4.7 %collective-permute-start.17 = (bf16[256,64]{0,1:T(8,128)(2,1)S(1)}, bf16[256,64]{0,1:T(8,128)(2,1)S(1)}, u32[]{:S(2)}, u32[]{:S(2)}) collective-permute-start(bf16[256,64]{0,1:T(8,128)(2,1)S(1)} %slice.262), channel_id=1, source_target_pairs={{2,0},{4,2},{6,4},{8,6},{10,8},{12,10},{14,12},{16,14},{18,16},{20... | collective-permute-start | bytes 98312 | tf_op jit(solution)/shard_map/ppermute | solution.py:13
  173.8 3.6 %collective-permute-start.18 = (f32[64,64]{0,1:T(8,128)S(1)}, f32[64,64]{0,1:T(8,128)S(1)}, u32[]{:S(2)}, u32[]{:S(2)}) collective-permute-start(f32[64,64]{0,1:T(8,128)S(1)} %fusion.70), channel_id=1, source_target_pairs={{0,2},{2,0},{4,6},{6,4},{8,10},{10,8},{12,14},{14,12},{16,18},{18,... | collective-permute-start | bytes 49160 | tf_op jit(solution)/shard_map/ppermute | solution.py:18
  177.3 4.0 %collective-permute-start.20 = (f32[64,64]{0,1:T(8,128)S(1)}, f32[64,64]{0,1:T(8,128)S(1)}, u32[]{:S(2)}, u32[]{:S(2)}) collective-permute-start(f32[64,64]{0,1:T(8,128)S(1)} %add.196), channel_id=1, source_target_pairs={{0,8},{2,10},{4,12},{6,14},{8,0},{10,2},{12,4},{14,6},{16,24},{18,... | collective-permute-start | bytes 49160 | tf_op jit(solution)/shard_map/ppermute | solution.py:18
  178.7 5.0 %collective-permute-start.21 = (f32[64,64]{0,1:T(8,128)S(1)}, f32[64,64]{0,1:T(8,128)S(1)}, u32[]{:S(2)}, u32[]{:S(2)}) collective-permute-start(f32[64,64]{0,1:T(8,128)S(1)} %add.196), channel_id=1, source_target_pairs={{0,12},{2,14},{4,8},{6,10},{8,4},{10,6},{12,0},{14,2},{16,28},{18,... | collective-permute-start | bytes 49160 | tf_op jit(solution)/shard_map/ppermute | solution.py:18
  181.4 3.9 %collective-permute-start.19 = (f32[64,64]{0,1:T(8,128)S(1)}, f32[64,64]{0,1:T(8,128)S(1)}, u32[]{:S(2)}, u32[]{:S(2)}) collective-permute-start(f32[64,64]{0,1:T(8,128)S(1)} %add.196), channel_id=1, source_target_pairs={{0,4},{2,6},{4,0},{6,2},{8,12},{10,14},{12,8},{14,10},{16,20},{18,... | collective-permute-start | bytes 49160 | tf_op jit(solution)/shard_map/ppermute | solution.py:18
  185.3 4.9 %collective-permute-start.22 = (f32[64,64]{0,1:T(8,128)S(1)}, f32[64,64]{0,1:T(8,128)S(1)}, u32[]{:S(2)}, u32[]{:S(2)}) collective-permute-start(f32[64,64]{0,1:T(8,128)S(1)} %add_add_fusion), channel_id=1, source_target_pairs={{0,16},{2,18},{4,20},{6,22},{8,24},{10,26},{12,28},{14,30},{16,0},... | collective-permute-start | bytes 49160 | tf_op jit(solution)/shard_map/ppermute | solution.py:18
  (15 other events, 148.9 us)
where the time goes:
time: 204 us; the launch traced here: 203 us
  other arithmetic  70.1 us (34%)
  waiting for transfers between devices  42.8 us (21%)
  starting transfers between devices  42.4 us (21%)
  local copies, waits for them, and re-layouts  32.8 us (16%)
  blocking collectives  8.99 us (4%)
  matrix products  5.26 us (3%)
    gather x13, local copies, waits for them, and re-layouts, on_device(): picked = jnp.take(window, safe_slots[:, offset], axis=1)  32.4 us
    ppermute x15, starting transfers between devices, exchanged(): return lax.ppermute(value, axis, [(i, i ^ distance) for i in range(count)])  24.7 us
    ppermute x15, waiting for transfers between devices, exchanged(): return lax.ppermute(value, axis, [(i, i ^ distance) for i in range(count)])  24.7 us
    dot_general x2, other arithmetic, on_device(): jnp.einsum('svf,svf->v', zscored, picked, preferred_element_type=jnp.floa...  24.1 us
    another operation x9, other arithmetic, orthonormal(): factor = jnp.linalg.cholesky(gram_matrix)  19.6 us
    ppermute x8, waiting for transfers between devices, shifted(): return lax.ppermute(shard, axis, pairs)  18.2 us
    ppermute x8, starting transfers between devices, shifted(): return lax.ppermute(shard, axis, pairs)  17.7 us
    another operation x6, other arithmetic, orthonormal(): lax.linalg.triangular_solve(factor, images, left_side=False, lower=True,...  16.6 us
  transfers between devices with their start and end apart: 23, of which 16 were waited for; matrix products, arithmetic and copies ran while one was open for 2% of the time, Pallas kernels for 0%

commit v1 on v0

--- a/solution.py
+++ b/solution.py
@@ -84,7 +84,7 @@
             jnp.einsum("svf,svf->v", zscored, picked, preferred_element_type=jnp.float32)
         )
     partial_sums = jnp.stack(columns, axis=1)
-    summed = lax.psum(partial_sums, "subj")
+    summed = jnp.sum(lax.all_gather(partial_sums, "subj"), axis=0)
     weight = jnp.where(present, jnp.exp(scale_factor * summed), 0.0)
     living = live_mask.astype(jnp.float32)
     local_graph = dense_graph(weight, neighbours, 2 * voxels_here)

time: 204 us -> 200 us (0.980)
  blocking collectives: 8.99 us -> 4.7 us
    psum x1 -> x0, blocking collectives: 8.99 us -> none  [on_device(): summed = lax.psum(partial_sums, 'subj')]
    all_gather x0 -> x1, blocking collectives: none -> 4.7 us  [on_device(): summed = jnp.sum(lax.all_gather(partial_sums, 'subj'), axis=0)]
where the time goes in v1:
time: 200 us
  other arithmetic  70.1 us (35%)
  waiting for transfers between devices  44.2 us (22%)
  starting transfers between devices  41.5 us (21%)
  local copies, waits for them, and re-layouts  32.8 us (16%)
  matrix products  5.26 us (3%)
  blocking collectives  4.7 us (2%)
    gather x13, local copies, waits for them, and re-layouts, on_device(): picked = jnp.take(window, safe_slots[:, offset], axis=1)  32.4 us
    ppermute x15, starting transfers between devices, exchanged(): return lax.ppermute(value, axis, [(i, i ^ distance) for i in range(count)])  24.7 us
    ppermute x15, waiting for transfers between devices, exchanged(): return lax.ppermute(value, axis, [(i, i ^ distance) for i in range(count)])  24.7 us
    dot_general x2, other arithmetic, on_device(): jnp.einsum('svf,svf->v', zscored, picked, preferred_element_type=jnp.floa...  24.1 us
    another operation x9, other arithmetic, orthonormal(): factor = jnp.linalg.cholesky(gram_matrix)  19.6 us
    ppermute x8, waiting for transfers between devices, shifted(): return lax.ppermute(shard, axis, pairs)  19.6 us
    ppermute x8, starting transfers between devices, shifted(): return lax.ppermute(shard, axis, pairs)  16.8 us
    another operation x6, other arithmetic, orthonormal(): lax.linalg.triangular_solve(factor, images, left_side=False, lower=True,...  16.6 us
  transfers between devices with their start and end apart: 23, of which 16 were waited for; matrix products, arithmetic and copies ran while one was open for 2% of the time, Pallas kernels for 0%

profile of v1, /device:TPU:0, one launch (start us, length us, event | category | flops | bytes accessed | tf_op | source)
XLA Modules:
  0.0 199.6 jit_solution(2422159553742714288)
XLA Ops:
  5.0 2.6 %collective-permute-start = (bf16[4,256,512]{2,0,1:T(4,128)(2,1)S(1)}, bf16[4,256,512]{2,0,1:T(4,128)(2,1)S(1)}, u32[]{:S(2)}, u32[]{:S(2)}) collective-permute-start(bf16[4,256,512]{2,0,1:T(4,128)(2,1)S(1)} %fusion.3), channel_id=1, source_target_pairs={{0,2},{2,4},{4,6},{6,8},{8,10},{10,12},{12,14},{14,16},{16,18},{18... | collective-permute-start | bytes 3145736 | tf_op jit(solution)/shard_map/ppermute | solution.py:13
  21.5 2.5 %gather_fusion.12 = bf16[256,4,512]{2,1,0:T(4,128)(2,1)} fusion(bf16[4,512,512]{2,0,1:T(4,128)(2,1)S(1)} %pad_maximum_fusion, s32[1024]{0:T(1024)S(1)} %pad_clamp_fusion), kind=kCustom, calls=%fused_computation.12.clone | custom fusion | bytes 2098176 | tf_op jit(solution)/shard_map/jit(_take)/gather | solution.py:82
  36.4 2.7 %gather_fusion.6 = bf16[256,4,512]{2,1,0:T(4,128)(2,1)} fusion(bf16[4,512,512]{2,0,1:T(4,128)(2,1)S(1)} %pad_maximum_fusion, s32[1024]{0:T(1024)S(1)} %pad_clamp_fusion.6), kind=kCustom, calls=%fused_computation.6.clone | custom fusion | bytes 2098176 | tf_op jit(solution)/shard_map/jit(_take)/gather | solution.py:82
  44.1 9.5 %fusion.7 = (f32[256]{0:T(256)S(1)}, f32[256]{0:T(256)S(1)}, f32[256]{0:T(256)S(1)}, f32[256]{0:T(256)S(1)}) fusion(bf16[256,4,512]{2,1,0:T(4,128)(2,1)} %gather_fusion.3, pred[256]{0:T(512)(128)(4,1)S(1)} %get-tuple-element.72, bf16[256,4,512]{2,1,0:T(4,128)(2,1)} %gather_fusion.2, pred[256]{0:T(512)(128)(4,1)S(1)} %get-tuple-element.73, ...), kind=kLoop, calls=%fused_computation.35 | loop fusion | flops 11009024 | bytes 5256192 | tf_op jit(solution)/shard_map/svf,svf->v/dot_general | solution.py:84
  53.7 14.7 %fusion.16 = (f32[256]{0:T(256)S(1)}, f32[256]{0:T(256)S(1)}, f32[256]{0:T(256)S(1)}, f32[256]{0:T(256)S(1)}, f32[256]{0:T(256)S(1)}, /*index=5*/f32[256]{0:T(25...) fusion(bf16[256,4,512]{2,1,0:T(4,128)(2,1)S(1)} %copy-done.1, pred[256]{0:T(512)(128)(4,1)S(1)} %get-tuple-element.76, ...), kind=kLoop, calls=%fused_computation.44 | loop fusion | flops 21493504 | bytes 10505472 | tf_op jit(solution)/shard_map/svf,svf->v/dot_general | solution.py:84
  68.5 4.7 %all-gather = f32[512,13]{0,1:T(8,128)S(1)} all-gather(f32[256,13]{0,1:T(8,128)S(1)} %stack.55), channel_id=2, replica_groups=mesh['vox'=16,'subj'=2] {'subj'}, dimensions={0}, use_global_device_ids=true | all-gather | bytes 39936 | tf_op jit(solution)/shard_map/all_gather | solution.py:87
  75.6 11.2 %collective-permute-done.1 = f32[256]{0:T(256)S(1)} collective-permute-done((f32[256]{0:T(256)S(1)}, f32[256]{0:T(256)S(1)}, u32[]{:S(2)}, u32[]{:S(2)}) %collective-permute-start.1) | collective-permute-done | bytes 1056 | tf_op jit(solution)/shard_map/ppermute | solution.py:13
  86.8 6.2 %collective-permute-start.2 = (bf16[256,64]{0,1:T(8,128)(2,1)S(1)}, bf16[256,64]{0,1:T(8,128)(2,1)S(1)}, u32[]{:S(2)}, u32[]{:S(2)}) collective-permute-start(bf16[256,64]{0,1:T(8,128)(2,1)S(1)} %get-tuple-element.25), channel_id=1, source_target_pairs={{0,2},{2,4},{4,6},{6,8},{8,10},{10,12},{12,14},{14,16},{16,18},{18... | collective-permute-start | bytes 98312 | tf_op jit(solution)/shard_map/ppermute | solution.py:13
  97.4 2.9 %collective-permute-start.4 = (f32[64,64]{0,1:T(8,128)S(1)}, f32[64,64]{0,1:T(8,128)S(1)}, u32[]{:S(2)}, u32[]{:S(2)}) collective-permute-start(f32[64,64]{0,1:T(8,128)S(1)} %fusion.66), channel_id=1, source_target_pairs={{0,2},{2,0},{4,6},{6,4},{8,10},{10,8},{12,14},{14,12},{16,18},{18,... | collective-permute-start | bytes 49160 | tf_op jit(solution)/shard_map/ppermute | solution.py:18
  109.2 2.7 %collective-permute-start.8 = (f32[64,64]{0,1:T(8,128)S(1)}, f32[64,64]{0,1:T(8,128)S(1)}, u32[]{:S(2)}, u32[]{:S(2)}) collective-permute-start(f32[64,64]{0,1:T(8,128)S(1)} %add_add_fusion.2), channel_id=1, source_target_pairs={{0,16},{2,18},{4,20},{6,22},{8,24},{10,26},{12,28},{14,30},{16,0},... | collective-permute-start | bytes 49160 | tf_op jit(solution)/shard_map/ppermute | solution.py:18
  114.1 5.8 %cholesky.59 = f32[64,64]{1,0:T(8,128)S(1)} custom-call(f32[64,64]{1,0:T(8,128)S(1)} %fusion.49), custom_call_target="Cholesky" | custom-call | tf_op jit(solution)/shard_map/jit(cholesky)/cholesky | solution.py:51
  121.3 4.9 %custom-call.7 = f32[1,64,64]{1,2,0:T(8,128)S(1)} custom-call(f32[1,64,64]{2,1,0:T(8,128)S(1)} %fusion.41), custom_call_target="InvertDiagBlocksLowerTriangular" | custom-call | tf_op jit(solution)/shard_map/triangular_solve/custom-call.0 | solution.py:52
  129.9 3.2 %collective-permute-done.10 = bf16[256,64]{0,1:T(8,128)(2,1)S(1)} collective-permute-done((bf16[256,64]{0,1:T(8,128)(2,1)S(1)}, bf16[256,64]{0,1:T(8,128)(2,1)S(1)}, u32[]{:S(2)}, u32[]{:S(2)}) %collective-permute-start.10) | collective-permute-done | bytes 32800 | tf_op jit(solution)/shard_map/ppermute | solution.py:13
  133.9 2.7 %collective-permute-start.11 = (f32[64,64]{0,1:T(8,128)S(1)}, f32[64,64]{0,1:T(8,128)S(1)}, u32[]{:S(2)}, u32[]{:S(2)}) collective-permute-start(f32[64,64]{0,1:T(8,128)S(1)} %fusion.68), channel_id=1, source_target_pairs={{0,2},{2,0},{4,6},{6,4},{8,10},{10,8},{12,14},{14,12},{16,18},{18,... | collective-permute-start | bytes 49160 | tf_op jit(solution)/shard_map/ppermute | solution.py:18
  138.8 2.7 %collective-permute-start.14 = (f32[64,64]{0,1:T(8,128)S(1)}, f32[64,64]{0,1:T(8,128)S(1)}, u32[]{:S(2)}, u32[]{:S(2)}) collective-permute-start(f32[64,64]{0,1:T(8,128)S(1)} %add.185), channel_id=1, source_target_pairs={{0,12},{2,14},{4,8},{6,10},{8,4},{10,6},{12,0},{14,2},{16,28},{18,... | collective-permute-start | bytes 49160 | tf_op jit(solution)/shard_map/ppermute | solution.py:18
  146.6 3.7 %collective-permute-done.15 = f32[64,64]{0,1:T(8,128)S(1)} collective-permute-done((f32[64,64]{0,1:T(8,128)S(1)}, f32[64,64]{0,1:T(8,128)S(1)}, u32[]{:S(2)}, u32[]{:S(2)}) %collective-permute-start.15) | collective-permute-done | bytes 16416 | tf_op jit(solution)/shard_map/ppermute | solution.py:18
  150.4 5.8 %cholesky.70 = f32[64,64]{1,0:T(8,128)S(1)} custom-call(f32[64,64]{1,0:T(8,128)S(1)} %fusion.47), custom_call_target="Cholesky" | custom-call | tf_op jit(solution)/shard_map/jit(cholesky)/cholesky | solution.py:51
  157.6 4.9 %custom-call.8 = f32[1,64,64]{1,2,0:T(8,128)S(1)} custom-call(f32[1,64,64]{2,1,0:T(8,128)S(1)} %fusion.42), custom_call_target="InvertDiagBlocksLowerTriangular" | custom-call | tf_op jit(solution)/shard_map/triangular_solve/custom-call.0 | solution.py:52
  165.9 3.4 %collective-permute-done.17 = bf16[256,64]{0,1:T(8,128)(2,1)S(1)} collective-permute-done((bf16[256,64]{0,1:T(8,128)(2,1)S(1)}, bf16[256,64]{0,1:T(8,128)(2,1)S(1)}, u32[]{:S(2)}, u32[]{:S(2)}) %collective-permute-start.17) | collective-permute-done | bytes 32800 | tf_op jit(solution)/shard_map/ppermute | solution.py:13
  170.1 2.7 %collective-permute-start.18 = (f32[64,64]{0,1:T(8,128)S(1)}, f32[64,64]{0,1:T(8,128)S(1)}, u32[]{:S(2)}, u32[]{:S(2)}) collective-permute-start(f32[64,64]{0,1:T(8,128)S(1)} %fusion.70), channel_id=1, source_target_pairs={{0,2},{2,0},{4,6},{6,4},{8,10},{10,8},{12,14},{14,12},{16,18},{18,... | collective-permute-start | bytes 49160 | tf_op jit(solution)/shard_map/ppermute | solution.py:18
  175.0 2.7 %collective-permute-start.21 = (f32[64,64]{0,1:T(8,128)S(1)}, f32[64,64]{0,1:T(8,128)S(1)}, u32[]{:S(2)}, u32[]{:S(2)}) collective-permute-start(f32[64,64]{0,1:T(8,128)S(1)} %add.194), channel_id=1, source_target_pairs={{0,12},{2,14},{4,8},{6,10},{8,4},{10,6},{12,0},{14,2},{16,28},{18,... | collective-permute-start | bytes 49160 | tf_op jit(solution)/shard_map/ppermute | solution.py:18
  181.7 4.8 %collective-permute-done.22 = f32[64,64]{0,1:T(8,128)S(1)} collective-permute-done((f32[64,64]{0,1:T(8,128)S(1)}, f32[64,64]{0,1:T(8,128)S(1)}, u32[]{:S(2)}, u32[]{:S(2)}) %collective-permute-start.22) | collective-permute-done | bytes 16416 | tf_op jit(solution)/shard_map/ppermute | solution.py:18
  186.6 5.8 %cholesky.81 = f32[64,64]{1,0:T(8,128)S(1)} custom-call(f32[64,64]{1,0:T(8,128)S(1)} %fusion.45), custom_call_target="Cholesky" | custom-call | tf_op jit(solution)/shard_map/jit(cholesky)/cholesky | solution.py:51
  193.8 4.9 %custom-call.9 = f32[1,64,64]{1,2,0:T(8,128)S(1)} custom-call(f32[1,64,64]{2,1,0:T(8,128)S(1)} %fusion.43), custom_call_target="InvertDiagBlocksLowerTriangular" | custom-call | tf_op jit(solution)/shard_map/triangular_solve/custom-call.0 | solution.py:52
  (170 shorter events, 80.8 us)
Async XLA Ops:
  5.0 5.2 %collective-permute-start = (bf16[4,256,512]{2,0,1:T(4,128)(2,1)S(1)}, bf16[4,256,512]{2,0,1:T(4,128)(2,1)S(1)}, u32[]{:S(2)}, u32[]{:S(2)}) collective-permute-start(bf16[4,256,512]{2,0,1:T(4,128)(2,1)S(1)} %fusion.3), channel_id=1, source_target_pairs={{0,2},{2,4},{4,6},{6,8},{8,10},{10,12},{12,14},{14,16},{16,18},{18... | collective-permute-start | bytes 3145736 | tf_op jit(solution)/shard_map/ppermute | solution.py:13
  53.7 33.0 %copy-start.6 = (f32[256,64]{0,1:T(8,128)S(1)}, f32[256,64]{0,1:T(8,128)}, u32[]{:S(2)}) copy-start(f32[256,64]{0,1:T(8,128)} %param.12) | copy-start | bytes 196612
  74.2 12.5 %collective-permute-start.1 = (f32[256]{0:T(256)S(1)}, f32[256]{0:T(256)S(1)}, u32[]{:S(2)}, u32[]{:S(2)}) collective-permute-start(f32[256]{0:T(256)S(1)} %slice.190), channel_id=1, source_target_pairs={{2,0},{4,2},{6,4},{8,6},{10,8},{12,10},{14,12},{16,14},{18,16},{20... | collective-permute-start | bytes 3080 | tf_op jit(solution)/shard_map/ppermute | solution.py:13
  86.8 8.0 %collective-permute-start.2 = (bf16[256,64]{0,1:T(8,128)(2,1)S(1)}, bf16[256,64]{0,1:T(8,128)(2,1)S(1)}, u32[]{:S(2)}, u32[]{:S(2)}) collective-permute-start(bf16[256,64]{0,1:T(8,128)(2,1)S(1)} %get-tuple-element.25), channel_id=1, source_target_pairs={{0,2},{2,4},{4,6},{6,8},{8,10},{10,12},{12,14},{14,16},{16,18},{18... | collective-permute-start | bytes 98312 | tf_op jit(solution)/shard_map/ppermute | solution.py:13
  93.4 3.1 %collective-permute-start.3 = (bf16[256,64]{0,1:T(8,128)(2,1)S(1)}, bf16[256,64]{0,1:T(8,128)(2,1)S(1)}, u32[]{:S(2)}, u32[]{:S(2)}) collective-permute-start(bf16[256,64]{0,1:T(8,128)(2,1)S(1)} %slice.264), channel_id=1, source_target_pairs={{2,0},{4,2},{6,4},{8,6},{10,8},{12,10},{14,12},{16,14},{18,16},{20... | collective-permute-start | bytes 98312 | tf_op jit(solution)/shard_map/ppermute | solution.py:13
  97.4 3.8 %collective-permute-start.4 = (f32[64,64]{0,1:T(8,128)S(1)}, f32[64,64]{0,1:T(8,128)S(1)}, u32[]{:S(2)}, u32[]{:S(2)}) collective-permute-start(f32[64,64]{0,1:T(8,128)S(1)} %fusion.66), channel_id=1, source_target_pairs={{0,2},{2,0},{4,6},{6,4},{8,10},{10,8},{12,14},{14,12},{16,18},{18,... | collective-permute-start | bytes 49160 | tf_op jit(solution)/shard_map/ppermute | solution.py:18
  101.2 4.2 %collective-permute-start.6 = (f32[64,64]{0,1:T(8,128)S(1)}, f32[64,64]{0,1:T(8,128)S(1)}, u32[]{:S(2)}, u32[]{:S(2)}) collective-permute-start(f32[64,64]{0,1:T(8,128)S(1)} %add.176), channel_id=1, source_target_pairs={{0,8},{2,10},{4,12},{6,14},{8,0},{10,2},{12,4},{14,6},{16,24},{18,... | collective-permute-start | bytes 49160 | tf_op jit(solution)/shard_map/ppermute | solution.py:18
  102.9 4.8 %collective-permute-start.7 = (f32[64,64]{0,1:T(8,128)S(1)}, f32[64,64]{0,1:T(8,128)S(1)}, u32[]{:S(2)}, u32[]{:S(2)}) collective-permute-start(f32[64,64]{0,1:T(8,128)S(1)} %add.176), channel_id=1, source_target_pairs={{0,12},{2,14},{4,8},{6,10},{8,4},{10,6},{12,0},{14,2},{16,28},{18,... | collective-permute-start | bytes 49160 | tf_op jit(solution)/shard_map/ppermute | solution.py:18
  105.2 3.9 %collective-permute-start.5 = (f32[64,64]{0,1:T(8,128)S(1)}, f32[64,64]{0,1:T(8,128)S(1)}, u32[]{:S(2)}, u32[]{:S(2)}) collective-permute-start(f32[64,64]{0,1:T(8,128)S(1)} %add.176), channel_id=1, source_target_pairs={{0,4},{2,6},{4,0},{6,2},{8,12},{10,14},{12,8},{14,10},{16,20},{18,... | collective-permute-start | bytes 49160 | tf_op jit(solution)/shard_map/ppermute | solution.py:18
  109.2 4.9 %collective-permute-start.8 = (f32[64,64]{0,1:T(8,128)S(1)}, f32[64,64]{0,1:T(8,128)S(1)}, u32[]{:S(2)}, u32[]{:S(2)}) collective-permute-start(f32[64,64]{0,1:T(8,128)S(1)} %add_add_fusion.2), channel_id=1, source_target_pairs={{0,16},{2,18},{4,20},{6,22},{8,24},{10,26},{12,28},{14,30},{16,0},... | collective-permute-start | bytes 49160 | tf_op jit(solution)/shard_map/ppermute | solution.py:18
  126.5 3.3 %collective-permute-start.9 = (bf16[256,64]{0,1:T(8,128)(2,1)S(1)}, bf16[256,64]{0,1:T(8,128)(2,1)S(1)}, u32[]{:S(2)}, u32[]{:S(2)}) collective-permute-start(bf16[256,64]{0,1:T(8,128)(2,1)S(1)} %get-tuple-element.23), channel_id=1, source_target_pairs={{0,2},{2,4},{4,6},{6,8},{8,10},{10,12},{12,14},{14,16},{16,18},{18... | collective-permute-start | bytes 98312 | tf_op jit(solution)/shard_map/ppermute | solution.py:13
  128.3 4.8 %collective-permute-start.10 = (bf16[256,64]{0,1:T(8,128)(2,1)S(1)}, bf16[256,64]{0,1:T(8,128)(2,1)S(1)}, u32[]{:S(2)}, u32[]{:S(2)}) collective-permute-start(bf16[256,64]{0,1:T(8,128)(2,1)S(1)} %slice.263), channel_id=1, source_target_pairs={{2,0},{4,2},{6,4},{8,6},{10,8},{12,10},{14,12},{16,14},{18,16},{20... | collective-permute-start | bytes 98312 | tf_op jit(solution)/shard_map/ppermute | solution.py:13
  133.9 3.6 %collective-permute-start.11 = (f32[64,64]{0,1:T(8,128)S(1)}, f32[64,64]{0,1:T(8,128)S(1)}, u32[]{:S(2)}, u32[]{:S(2)}) collective-permute-start(f32[64,64]{0,1:T(8,128)S(1)} %fusion.68), channel_id=1, source_target_pairs={{0,2},{2,0},{4,6},{6,4},{8,10},{10,8},{12,14},{14,12},{16,18},{18,... | collective-permute-start | bytes 49160 | tf_op jit(solution)/shard_map/ppermute | solution.py:18
  137.5 4.1 %collective-permute-start.13 = (f32[64,64]{0,1:T(8,128)S(1)}, f32[64,64]{0,1:T(8,128)S(1)}, u32[]{:S(2)}, u32[]{:S(2)}) collective-permute-start(f32[64,64]{0,1:T(8,128)S(1)} %add.185), channel_id=1, source_target_pairs={{0,8},{2,10},{4,12},{6,14},{8,0},{10,2},{12,4},{14,6},{16,24},{18,... | collective-permute-start | bytes 49160 | tf_op jit(solution)/shard_map/ppermute | solution.py:18
  138.8 5.0 %collective-permute-start.14 = (f32[64,64]{0,1:T(8,128)S(1)}, f32[64,64]{0,1:T(8,128)S(1)}, u32[]{:S(2)}, u32[]{:S(2)}) collective-permute-start(f32[64,64]{0,1:T(8,128)S(1)} %add.185), channel_id=1, source_target_pairs={{0,12},{2,14},{4,8},{6,10},{8,4},{10,6},{12,0},{14,2},{16,28},{18,... | collective-permute-start | bytes 49160 | tf_op jit(solution)/shard_map/ppermute | solution.py:18
  141.5 3.9 %collective-permute-start.12 = (f32[64,64]{0,1:T(8,128)S(1)}, f32[64,64]{0,1:T(8,128)S(1)}, u32[]{:S(2)}, u32[]{:S(2)}) collective-permute-start(f32[64,64]{0,1:T(8,128)S(1)} %add.185), channel_id=1, source_target_pairs={{0,4},{2,6},{4,0},{6,2},{8,12},{10,14},{12,8},{14,10},{16,20},{18,... | collective-permute-start | bytes 49160 | tf_op jit(solution)/shard_map/ppermute | solution.py:18
  145.4 4.9 %collective-permute-start.15 = (f32[64,64]{0,1:T(8,128)S(1)}, f32[64,64]{0,1:T(8,128)S(1)}, u32[]{:S(2)}, u32[]{:S(2)}) collective-permute-start(f32[64,64]{0,1:T(8,128)S(1)} %add_add_fusion.1), channel_id=1, source_target_pairs={{0,16},{2,18},{4,20},{6,22},{8,24},{10,26},{12,28},{14,30},{16,0},... | collective-permute-start | bytes 49160 | tf_op jit(solution)/shard_map/ppermute | solution.py:18
  162.8 3.1 %collective-permute-start.16 = (bf16[256,64]{0,1:T(8,128)(2,1)S(1)}, bf16[256,64]{0,1:T(8,128)(2,1)S(1)}, u32[]{:S(2)}, u32[]{:S(2)}) collective-permute-start(bf16[256,64]{0,1:T(8,128)(2,1)S(1)} %get-tuple-element.21), channel_id=1, source_target_pairs={{0,2},{2,4},{4,6},{6,8},{8,10},{10,12},{12,14},{14,16},{16,18},{18... | collective-permute-start | bytes 98312 | tf_op jit(solution)/shard_map/ppermute | solution.py:13
  164.6 4.7 %collective-permute-start.17 = (bf16[256,64]{0,1:T(8,128)(2,1)S(1)}, bf16[256,64]{0,1:T(8,128)(2,1)S(1)}, u32[]{:S(2)}, u32[]{:S(2)}) collective-permute-start(bf16[256,64]{0,1:T(8,128)(2,1)S(1)} %slice.262), channel_id=1, source_target_pairs={{2,0},{4,2},{6,4},{8,6},{10,8},{12,10},{14,12},{16,14},{18,16},{20... | collective-permute-start | bytes 98312 | tf_op jit(solution)/shard_map/ppermute | solution.py:13
  170.1 3.6 %collective-permute-start.18 = (f32[64,64]{0,1:T(8,128)S(1)}, f32[64,64]{0,1:T(8,128)S(1)}, u32[]{:S(2)}, u32[]{:S(2)}) collective-permute-start(f32[64,64]{0,1:T(8,128)S(1)} %fusion.70), channel_id=1, source_target_pairs={{0,2},{2,0},{4,6},{6,4},{8,10},{10,8},{12,14},{14,12},{16,18},{18,... | collective-permute-start | bytes 49160 | tf_op jit(solution)/shard_map/ppermute | solution.py:18
  173.6 4.0 %collective-permute-start.20 = (f32[64,64]{0,1:T(8,128)S(1)}, f32[64,64]{0,1:T(8,128)S(1)}, u32[]{:S(2)}, u32[]{:S(2)}) collective-permute-start(f32[64,64]{0,1:T(8,128)S(1)} %add.194), channel_id=1, source_target_pairs={{0,8},{2,10},{4,12},{6,14},{8,0},{10,2},{12,4},{14,6},{16,24},{18,... | collective-permute-start | bytes 49160 | tf_op jit(solution)/shard_map/ppermute | solution.py:18
  175.0 5.0 %collective-permute-start.21 = (f32[64,64]{0,1:T(8,128)S(1)}, f32[64,64]{0,1:T(8,128)S(1)}, u32[]{:S(2)}, u32[]{:S(2)}) collective-permute-start(f32[64,64]{0,1:T(8,128)S(1)} %add.194), channel_id=1, source_target_pairs={{0,12},{2,14},{4,8},{6,10},{8,4},{10,6},{12,0},{14,2},{16,28},{18,... | collective-permute-start | bytes 49160 | tf_op jit(solution)/shard_map/ppermute | solution.py:18
  177.7 3.9 %collective-permute-start.19 = (f32[64,64]{0,1:T(8,128)S(1)}, f32[64,64]{0,1:T(8,128)S(1)}, u32[]{:S(2)}, u32[]{:S(2)}) collective-permute-start(f32[64,64]{0,1:T(8,128)S(1)} %add.194), channel_id=1, source_target_pairs={{0,4},{2,6},{4,0},{6,2},{8,12},{10,14},{12,8},{14,10},{16,20},{18,... | collective-permute-start | bytes 49160 | tf_op jit(solution)/shard_map/ppermute | solution.py:18
  181.6 4.9 %collective-permute-start.22 = (f32[64,64]{0,1:T(8,128)S(1)}, f32[64,64]{0,1:T(8,128)S(1)}, u32[]{:S(2)}, u32[]{:S(2)}) collective-permute-start(f32[64,64]{0,1:T(8,128)S(1)} %add_add_fusion), channel_id=1, source_target_pairs={{0,16},{2,18},{4,20},{6,22},{8,24},{10,26},{12,28},{14,30},{16,0},... | collective-permute-start | bytes 49160 | tf_op jit(solution)/shard_map/ppermute | solution.py:18
  (15 other events, 144.6 us)
